TPU v7x, 512 devices: a whole 4x8x8 slice. The times are simulated.
512 devices in a mesh: tm: 16 (over x_lo, y), stn: 32 (over x_hi, z, core).
Axes of the slice: x: 4 (x_hi: 2, x_lo: 2; x = x_hi * 2 + x_lo), y: 8, z: 8, core: 2. Of those that a mesh axis runs over, the one named last changes fastest.
Arguments:
- voltages: bfloat16 [2, 1024, 65536], P(None, 'stn', 'tm'), may hold values from -6 to 6
- filter_taps: float32 [12, 4096], replicated, may hold values from -1.75 to 1.75
- beam_weights: int32 [2, 512, 1024], P(None, 'stn'), may hold values from -32768 to 32767
- station_map: int32 [512], replicated, may hold values from 0 to 511, each once
- station_flags: int32 [512], replicated, may hold values 0 or 1
Outputs:
- beam_power: float32 [512, 16, 4096], P('stn', 'tm')
Inputs may be any that keep to these rules, and one draw needn't show every extreme that they name: `station_map`: each station number appears once.
All inputs are finite; a program needn't handle non-finite values.
Results may differ from a plain program's by a relative error of at most 0.0039.
Values may be sent and summed in bfloat16 or wider, within the bound.
No kernel may reach another device: no remote copies, remote signals or barrier semaphores. Data moves between devices by JAX's collectives and lax.ppermute only.
A program may use at most 64 MiB of HBM per device.

v0:
```python
import math

import jax
import jax.numpy as jnp
from jax import lax
from jax.sharding import PartitionSpec as P

RADIX = 64


exact_mode = lax.Precision.HIGHEST


def transform(real_in, imag_in, channels):
    index_row = jnp.arange(RADIX, dtype=jnp.int32)
    product = index_row[:, None] * index_row[None, :]
    angle_table = (product % RADIX).astype(jnp.float32) * (2.0 * math.pi / RADIX)
    cosine = jnp.cos(angle_table)
    sine_part = jnp.sin(angle_table)
    twiddle = product.astype(jnp.float32) * (2.0 * math.pi / channels)
    twiddle_cos = jnp.cos(twiddle)
    twiddle_sin = jnp.sin(twiddle)
    batch_rows = real_in.shape[0]
    real_cube = real_in.reshape(batch_rows, RADIX, RADIX)
    imag_cube = imag_in.reshape(batch_rows, RADIX, RADIX)
    mid_real = jnp.einsum("pab,ak->pbk", real_cube, cosine, precision=exact_mode) + jnp.einsum(
        "pab,ak->pbk", imag_cube, sine_part, precision=exact_mode
    )
    mid_imag = jnp.einsum("pab,ak->pbk", imag_cube, cosine, precision=exact_mode) - jnp.einsum(
        "pab,ak->pbk", real_cube, sine_part, precision=exact_mode
    )
    turn_real = mid_real * twiddle_cos + mid_imag * twiddle_sin
    turn_imag = mid_imag * twiddle_cos - mid_real * twiddle_sin
    out_real = jnp.einsum("pbk,bm->pmk", turn_real, cosine, precision=exact_mode) + jnp.einsum(
        "pbk,bm->pmk", turn_imag, sine_part, precision=exact_mode
    )
    out_imag = jnp.einsum("pbk,bm->pmk", turn_imag, cosine, precision=exact_mode) - jnp.einsum(
        "pbk,bm->pmk", turn_real, sine_part, precision=exact_mode
    )
    norm_scale = 1.0 / math.sqrt(channels)
    return (
        out_real.reshape(batch_rows, channels) * norm_scale,
        out_imag.reshape(batch_rows, channels) * norm_scale,
    )


def filter_spectra(extended, filter_taps, frame_count):
    inputs_here = extended.shape[1]
    channels = extended.shape[3]
    filtered = jnp.zeros((2, inputs_here, frame_count, channels), jnp.float32)
    for tap_index in range(filter_taps.shape[0]):
        filtered = filtered + filter_taps[tap_index] * extended[
            :, :, tap_index : tap_index + frame_count
        ].astype(jnp.float32)
    chan_real, chan_imag = transform(
        filtered[0].reshape(-1, channels), filtered[1].reshape(-1, channels), channels
    )
    return jnp.stack([chan_real.astype(jnp.bfloat16), chan_imag.astype(jnp.bfloat16)]).reshape(
        2, inputs_here, frame_count, channels
    )


def on_device(voltages, filter_taps, beam_weights, station_map, station_flags):
    local_inputs = voltages.shape[1]
    local_stations = local_inputs // 2
    stations = station_map.shape[0]
    channels = filter_taps.shape[1]
    history = filter_taps.shape[0] - 1
    first_slot = lax.axis_index("stn") * local_stations
    slot_ids = lax.dynamic_slice_in_dim(station_map, first_slot, local_stations)
    matches = slot_ids[:, None] == jnp.arange(stations, dtype=jnp.int32)[None, :]
    flag_slot = jnp.sum(jnp.where(matches, station_flags[None, :], 0), axis=1)
    keep_mask = jnp.repeat(flag_slot, 2).astype(jnp.bfloat16)
    masked = voltages * keep_mask[None, :, None]
    weight_int = beam_weights.reshape(2, beam_weights.shape[1], stations, 2)
    weight_int = jnp.take(weight_int, station_map, axis=2).reshape(
        2, beam_weights.shape[1], 2 * stations
    )
    weight_low = (weight_int.astype(jnp.float32) * (1.0 / 32768.0)).astype(jnp.bfloat16)
    weight_all = lax.all_gather(weight_low, "stn", axis=1, tiled=True)
    inputs_all = weight_all.shape[2]
    retiled = lax.all_to_all(masked, "tm", split_axis=1, concat_axis=2, tiled=True)
    few_inputs = retiled.shape[1]
    all_frames = retiled.shape[2] // channels
    frames = retiled.reshape(2, few_inputs, all_frames, channels)
    extended = jnp.concatenate(
        [jnp.zeros((2, few_inputs, history, channels), frames.dtype), frames], axis=2
    )
    spectra = filter_spectra(extended, filter_taps, all_frames)
    turned = lax.all_to_all(
        lax.all_to_all(spectra, "tm", split_axis=2, concat_axis=1, tiled=True),
        "stn",
        split_axis=3,
        concat_axis=1,
        tiled=True,
    )
    items = turned.shape[2]
    width = turned.shape[3]
    flat_real = turned[0].reshape(inputs_all, items * width)
    flat_imag = turned[1].reshape(inputs_all, items * width)
    beam_real = jnp.dot(weight_all[0], flat_real, preferred_element_type=jnp.float32) - jnp.dot(
        weight_all[1], flat_imag, preferred_element_type=jnp.float32
    )
    beam_imag = jnp.dot(weight_all[0], flat_imag, preferred_element_type=jnp.float32) + jnp.dot(
        weight_all[1], flat_real, preferred_element_type=jnp.float32
    )
    detected = (beam_real * beam_real + beam_imag * beam_imag) / inputs_all
    channel_power = detected.reshape(-1, items, width)
    return lax.all_to_all(channel_power, "stn", split_axis=0, concat_axis=2, tiled=True)


def solution(mesh):
    placed = (P(None, "stn", "tm"), P(), P(None, "stn", None), P(), P())
    return jax.shard_map(
        on_device, mesh=mesh, in_specs=placed, out_specs=P("stn", "tm", None), check_vma=False
    )
```

profile of v0, /device:TPU:1, one launch (start us, length us, event | category | flops | bytes accessed | tf_op | source)
XLA Modules:
  0.0 150.9 jit_solution(17499021985939143313)
XLA Ops:
  6.5 0.0 copy-start.2
  6.5 0.0 copy-start.1
  6.5 0.8 dynamic_slice.3
  7.4 0.9 select_reduce_fusion
  8.2 0.1 broadcast_in_dim.49
  8.3 0.1 convert_element_type.124
  8.4 2.5 %copy_multiply_fusion = bf16[2,32,4096]{2,0,1:T(2,128)(2,1)} fusion(bf16[2,32,4096]{2,1,0:T(8,128)(2,1)} %param.5, bf16[32]{0:T(256)(128)(2,1)S(1)} %convert_element_type.124), kind=kLoop, calls=%fused_computation.35 | loop fusion | flops 262144 | bytes 1048640 | tf_op jit(solution)/shard_map/mul | solution.py:74
  10.9 8.7 %all-to-all-start = ((bf16[2,32,4096]{2,0,1:T(2,128)(2,1)}), bf16[2,32,4096]{2,0,1:T(2,128)(2,1)S(1)}, u32[]{:S(2)}, u32[]{:S(2)}) async-start(bf16[2,32,4096]{2,0,1:T(2,128)(2,1)} %copy_multiply_fusion), calls=%async_computation | async-start | bytes 1048576 | tf_op jit(solution)/shard_map/all_to_all | solution.py:82
  19.6 0.0 all-gather.2.cloned.1.call-start
  19.6 0.0 copy-done.2
  19.7 0.1 broadcast_in_dim.42
  19.8 0.2 broadcast_in_dim.43
  20.0 0.0 copy-done.1
  20.0 0.3 copy.130
  20.3 2.8 %gather_fusion = s32[512,2,16,2]{2,3,1,0:T(2,128)S(1)} fusion(s32[2,16,512,2]{1,3,2,0:T(2,128)S(1)} %bitcast.84, s32[1024]{0:T(1024)S(1)} %pad_clamp_fusion), kind=kCustom, calls=%fused_computation | custom fusion | bytes 264192 | tf_op jit(solution)/shard_map/jit(_take)/gather | solution.py:76
  23.1 0.0 copy-start
  23.2 0.4 copy.131
  23.5 0.3 copy.132
  23.9 0.7 copy.133
  24.6 0.0 all-gather.2.cloned.1.call-update
  24.6 0.1 fusion.28
  24.7 0.1 copy.141
  24.8 0.1 fusion.27
  24.9 0.1 copy.146
  25.0 0.0 copy-done
  25.0 0.1 fusion.77
  25.2 7.7 %all-to-all-done = bf16[2,32,4096]{2,0,1:T(2,128)(2,1)S(1)} async-done(((bf16[2,32,4096]{2,0,1:T(2,128)(2,1)}), bf16[2,32,4096]{2,0,1:T(2,128)(2,1)S(1)}, u32[]{:S(2)}, u32[]{:S(2)}) %all-to-all-start) | async-done | bytes 524320 | tf_op jit(solution)/shard_map/all_to_all | solution.py:82
  32.9 0.3 copy.179
  33.2 1.6 %multiply_add_fusion.1 = f32[2,2,16,4096]{3,2,1,0:T(8,128)S(1)} fusion(bf16[2,2,16,4096]{3,2,1,0:T(8,128)(2,1)S(1)} %bitcast.88, f32[4096]{0:T(1024)S(1)} %bitcast.108, f32[4096]{0:T(1024)S(1)} %bitcast.109, f32[4096]{0:T(1024)S(1)} %bitcast.99, f32[4096]{0:T(1024)S(1)} %bitcast.100, f32[4096]{0:T(1024)S(1)} %bitcast.101, f32[4096]{0:T(1024)S(1)} %bitcast.102, ...), kind=kLoop, calls=%fused_computation.32 | loop fusion | flops 9175040 | bytes 1769472 | tf_op jit(solution)/shard_map/add | solution.py:52
  34.8 0.1 fusion.75
  34.8 0.4 reshape_reshape_squeeze.7
  35.3 0.4 reshape_reshape_squeeze.6
  35.7 1.8 %fusion.23 = f32[32,64,64]{2,1,0:T(8,128)S(1)} fusion(f32[32,64,64]{2,1,0:T(8,128)S(1)} %reshape_reshape_squeeze.6), kind=kOutput, calls=%fused_computation.53 | convolution fusion | flops 100720640 | bytes 1048576 | tf_op jit(solution)/shard_map/pab,ak->pbk/dot_general | solution.py:26
  37.5 1.8 %fusion.21 = f32[32,64,64]{2,1,0:T(8,128)S(1)} fusion(f32[32,64,64]{2,1,0:T(8,128)S(1)} %reshape_reshape_squeeze.7), kind=kOutput, calls=%fused_computation.51 | convolution fusion | flops 100720640 | bytes 1048576 | tf_op jit(solution)/shard_map/pab,ak->pbk/dot_general | solution.py:29
  39.3 1.8 %convolution_add_fusion.1 = f32[32,64,64]{2,1,0:T(8,128)S(1)} fusion(f32[32,64,64]{2,1,0:T(8,128)S(1)} %fusion.23, f32[32,64,64]{2,1,0:T(8,128)S(1)} %reshape_reshape_squeeze.7), kind=kOutput, calls=%fused_computation.17 | convolution fusion | flops 100851712 | bytes 1572864 | tf_op jit(solution)/shard_map/pab,ak->pbk/dot_general | solution.py:26
  41.2 1.8 %convolution_subtract_fusion.1 = f32[32,64,64]{2,1,0:T(8,128)S(1)} fusion(f32[32,64,64]{2,1,0:T(8,128)S(1)} %fusion.21, f32[32,64,64]{2,1,0:T(8,128)S(1)} %reshape_reshape_squeeze.6), kind=kOutput, calls=%fused_computation.16 | convolution fusion | flops 100851712 | bytes 1572864 | tf_op jit(solution)/shard_map/pab,ak->pbk/dot_general | solution.py:29
  43.0 1.2 fusion.13
  44.2 1.2 fusion.4
  45.3 0.5 convert_element_type.143
  45.8 0.6 copy.148
  46.4 1.4 fusion.12
  47.8 1.2 fusion.5
  49.0 0.5 convert_element_type.140
  49.4 0.6 copy.147
  50.0 1.2 pad_maximum_fusion
  51.2 18.2 %all_to_all.66 = bf16[2,2,16,4096]{3,0,1,2:T(2,128)(2,1)S(1)} all-to-all(bf16[2,2,16,4096]{3,0,1,2:T(2,128)(2,1)S(1)} %pad_maximum_fusion), channel_id=1, replica_groups=mesh['tm'=16,'stn'=32] {'tm'}, dimensions={2} | all-to-all | bytes 1048576 | tf_op jit(solution)/shard_map/all_to_all | solution.py:91
  69.4 1.6 %copy.149 = bf16[2,32,1,4096]{1,0,2,3:T(2,128)(2,1)S(1)} copy(bf16[2,32,1,4096]{3,0,1,2:T(2,128)(2,1)S(1)} %bitcast.90) | data formatting | bytes 1048576 | tf_op jit(solution)/shard_map/all_to_all | solution.py:91
  71.0 2.0 %reshape.122 = bf16[32,2,4096]{2,1,0:T(2,128)(2,1)S(1)} reshape(bf16[4096,1,2,32]{3,2,1,0:T(2,128)(2,1)S(1)} %bitcast.85) | data formatting | bytes 1048576
  73.0 37.8 %all_to_all.67 = bf16[32,2,4096]{2,1,0:T(2,128)(2,1)S(1)} all-to-all(bf16[32,2,4096]{2,1,0:T(2,128)(2,1)S(1)} %reshape.122), channel_id=1, replica_groups=mesh['tm'=16,'stn'=32] {'stn'}, dimensions={0} | all-to-all | bytes 1048576 | tf_op jit(solution)/shard_map/all_to_all | solution.py:90
  110.8 1.0 reshape.123
  111.9 1.2 copy.168
  113.1 0.1 copy.153
  113.2 0.1 copy.151
  113.3 4.6 %all-gather.2.cloned.1.call-done = bf16[2,512,1024]{2,0,1:T(2,128)(2,1)} async-done(((bf16[2,16,1024]{2,0,1:T(2,128)(2,1)}), bf16[2,512,1024]{2,0,1:T(2,128)(2,1)}) %all-gather.2.cloned.1.call-update) | async-done | bytes 2097168 | tf_op jit(solution)/shard_map/all_gather | solution.py:80
  118.0 5.6 %fusion.74 = (bf16[1,512,1024]{2,0,1:T(2,128)(2,1)S(1)}, bf16[1,512,1024]{2,0,1:T(2,128)(2,1)S(1)}) fusion(bf16[2,512,1024]{2,0,1:T(2,128)(2,1)} %all-gather.2.cloned.1.call-done), kind=kLoop, calls=%fused_computation.103 | loop fusion | bytes 4194304 | tf_op jit(solution)/shard_map/slice | solution.py:102
  123.5 0.4 fusion.10
  124.0 0.4 fusion.11
  124.4 0.4 fusion.9
  124.9 0.5 fusion.8
  125.4 17.9 %all_to_all.68 = f32[512,1,128]{2,1,0:T(1,128)S(1)} all-to-all(f32[512,1,128]{2,1,0:T(1,128)S(1)} %bitcast.95), channel_id=1, replica_groups=mesh['tm'=16,'stn'=32] {'stn'}, dimensions={0} | all-to-all | bytes 524288 | tf_op jit(solution)/shard_map/all_to_all | solution.py:109
  143.2 0.8 copy.155
  (6 shorter events, 0.1 us)
Async XLA Ops:
  6.5 13.1 %copy-start.2 = (s32[512]{0:T(512)S(1)}, s32[512]{0:T(512)}, u32[]{:S(2)}) copy-start(s32[512]{0:T(512)} %param.8) | copy-start | bytes 6148
  6.5 13.5 %copy-start.1 = (s32[2,16,1024]{2,1,0:T(8,128)S(1)}, s32[2,16,1024]{2,1,0:T(8,128)}, u32[]{:S(2)}) copy-start(s32[2,16,1024]{2,1,0:T(8,128)} %param.7) | copy-start | bytes 393220
  10.9 22.0 %all-to-all-start = ((bf16[2,32,4096]{2,0,1:T(2,128)(2,1)}), bf16[2,32,4096]{2,0,1:T(2,128)(2,1)S(1)}, u32[]{:S(2)}, u32[]{:S(2)}) async-start(bf16[2,32,4096]{2,0,1:T(2,128)(2,1)} %copy_multiply_fusion), calls=%async_computation | async-start | bytes 1048576 | tf_op jit(solution)/shard_map/all_to_all | solution.py:82
  19.6 98.4 %all-gather.2.cloned.1.call-start = ((), (), s32[]{:S(2)}) async-start(), calls=%async_computation.4 | async-start | bytes 2162688 | tf_op jit(solution)/shard_map/all_gather | solution.py:80
  23.1 1.9 %copy-start = (f32[12,4096]{1,0:T(8,128)S(1)}, f32[12,4096]{1,0:T(8,128)}, u32[]{:S(2)}) copy-start(f32[12,4096]{1,0:T(8,128)} %param.6) | copy-start | bytes 589828
Sparse Core Ops, SparseCore 0:
  24.7 93.2 all-gather.1
where the time goes:
time: 153 us; the launch traced here: 151 us
  blocking collectives  73.9 us (48%)
  local copies, waits for them, and re-layouts  21.8 us (14%)
  matrix products  14 us (9%)
  between operations  13.7 us (9%)
  waiting for transfers between devices  12.3 us (8%)
  starting transfers between devices  8.71 us (6%)
  other arithmetic  6.45 us (4%)
    all_to_all x1, blocking collectives, on_device(): lax.all_to_all(lax.all_to_all(spectra, 'tm', split_axis=2, concat_axis=1,...  37.8 us
    all_to_all x1, blocking collectives, on_device(): lax.all_to_all(spectra, 'tm', split_axis=2, concat_axis=1, tiled=True)  18.2 us
    all_to_all x1, blocking collectives, on_device(): lax.all_to_all(channel_power, 'stn', split_axis=0, concat_axis=2, tiled=T...  17.9 us
    all_to_all x1, starting transfers between devices, on_device(): lax.all_to_all(masked, 'tm', split_axis=1, concat_axis=2, tiled=True)  8.67 us
    all_to_all x1, waiting for transfers between devices, on_device(): lax.all_to_all(masked, 'tm', split_axis=1, concat_axis=2, tiled=True)  7.69 us
    slice x1, local copies, waits for them, and re-layouts, on_device(): weight_all[1]  5.55 us
    all_gather x1, waiting for transfers between devices, on_device(): weight_all = lax.all_gather(weight_low, 'stn', axis=1, tiled=True)  4.64 us
    gather x3, local copies, waits for them, and re-layouts, on_device(): jnp.take(weight_int, station_map, axis=2)  3.45 us
  transfers between devices with their start and end apart: 2, of which 2 were waited for; matrix products, arithmetic and copies ran while one was open for 20% of the time, Pallas kernels for 0%

commit v1 on v0

--- a/solution.py
+++ b/solution.py
@@ -9,6 +9,17 @@
 
 
 exact_mode = lax.Precision.HIGHEST
+
+BOTH = ("tm", "stn")
+
+
+def stn_index(xhi, z, core):
+    return xhi * 16 + z * 2 + core
+
+
+Z_GROUPS = [[stn_index(xhi, z, core) for z in range(8)] for xhi in range(2) for core in range(2)]
+SWAP_XHI = [(i, i ^ 16) for i in range(32)]
+SWAP_CORE = [(i, i ^ 1) for i in range(32)]
 
 
 def transform(real_in, imag_in, channels):
@@ -60,26 +71,35 @@
     )
 
 
+def local_weights(beam_weights, station_map, station_flags):
+    beams = beam_weights.shape[1]
+    inputs = beam_weights.shape[2]
+    order = station_map.reshape(32, 16).T.reshape(-1)
+    target = (2 * order[:, None] + jnp.arange(2, dtype=jnp.int32)[None, :]).reshape(-1)
+    keep = jnp.repeat(station_flags, 2)
+    rows = jnp.arange(inputs, dtype=jnp.int32)
+    select = ((rows[:, None] == target[None, :]) & (keep[:, None] > 0)).astype(jnp.bfloat16)
+    weight_low = (beam_weights.astype(jnp.float32) * (1.0 / 32768.0)).astype(jnp.bfloat16)
+    return jnp.dot(
+        weight_low.reshape(2 * beams, inputs), select, preferred_element_type=jnp.float32
+    ).astype(jnp.bfloat16)
+
+
+def block_power(weights, spectra, inputs_all):
+    product = jnp.dot(weights, spectra, preferred_element_type=jnp.float32)
+    product = product.reshape(8, 2, 16, 2, 128)
+    beam_real = product[:, 0, :, 0] - product[:, 1, :, 1]
+    beam_imag = product[:, 0, :, 1] + product[:, 1, :, 0]
+    return ((beam_real * beam_real + beam_imag * beam_imag) / inputs_all).astype(jnp.bfloat16)
+
+
 def on_device(voltages, filter_taps, beam_weights, station_map, station_flags):
-    local_inputs = voltages.shape[1]
-    local_stations = local_inputs // 2
-    stations = station_map.shape[0]
     channels = filter_taps.shape[1]
     history = filter_taps.shape[0] - 1
-    first_slot = lax.axis_index("stn") * local_stations
-    slot_ids = lax.dynamic_slice_in_dim(station_map, first_slot, local_stations)
-    matches = slot_ids[:, None] == jnp.arange(stations, dtype=jnp.int32)[None, :]
-    flag_slot = jnp.sum(jnp.where(matches, station_flags[None, :], 0), axis=1)
-    keep_mask = jnp.repeat(flag_slot, 2).astype(jnp.bfloat16)
-    masked = voltages * keep_mask[None, :, None]
-    weight_int = beam_weights.reshape(2, beam_weights.shape[1], stations, 2)
-    weight_int = jnp.take(weight_int, station_map, axis=2).reshape(
-        2, beam_weights.shape[1], 2 * stations
-    )
-    weight_low = (weight_int.astype(jnp.float32) * (1.0 / 32768.0)).astype(jnp.bfloat16)
-    weight_all = lax.all_gather(weight_low, "stn", axis=1, tiled=True)
-    inputs_all = weight_all.shape[2]
-    retiled = lax.all_to_all(masked, "tm", split_axis=1, concat_axis=2, tiled=True)
+    inputs_all = beam_weights.shape[2]
+    retiled = lax.all_to_all(voltages, "tm", split_axis=1, concat_axis=2, tiled=True)
+    own = local_weights(beam_weights, station_map, station_flags)
+    gathered = lax.all_gather(own, "stn", axis=0, tiled=True, axis_index_groups=Z_GROUPS)
     few_inputs = retiled.shape[1]
     all_frames = retiled.shape[2] // channels
     frames = retiled.reshape(2, few_inputs, all_frames, channels)
@@ -87,26 +107,23 @@
         [jnp.zeros((2, few_inputs, history, channels), frames.dtype), frames], axis=2
     )
     spectra = filter_spectra(extended, filter_taps, all_frames)
-    turned = lax.all_to_all(
-        lax.all_to_all(spectra, "tm", split_axis=2, concat_axis=1, tiled=True),
-        "stn",
-        split_axis=3,
-        concat_axis=1,
-        tiled=True,
+    outgoing = spectra.reshape(2, 2, 16, 32, 128).transpose(2, 3, 1, 0, 4).reshape(512, 2, 256)
+    turned = lax.all_to_all(outgoing, BOTH, split_axis=0, concat_axis=0, tiled=True)
+    turned = turned.reshape(inputs_all, 256)
+    other_core = lax.ppermute(gathered, "stn", SWAP_CORE)
+    other_xhi = lax.ppermute(gathered, "stn", SWAP_XHI)
+    other_both = lax.ppermute(other_xhi, "stn", SWAP_CORE)
+    power = jnp.stack(
+        [
+            jnp.stack([block_power(gathered, turned, inputs_all), block_power(other_core, turned, inputs_all)], 1),
+            jnp.stack([block_power(other_xhi, turned, inputs_all), block_power(other_both, turned, inputs_all)], 1),
+        ]
     )
-    items = turned.shape[2]
-    width = turned.shape[3]
-    flat_real = turned[0].reshape(inputs_all, items * width)
-    flat_imag = turned[1].reshape(inputs_all, items * width)
-    beam_real = jnp.dot(weight_all[0], flat_real, preferred_element_type=jnp.float32) - jnp.dot(
-        weight_all[1], flat_imag, preferred_element_type=jnp.float32
-    )
-    beam_imag = jnp.dot(weight_all[0], flat_imag, preferred_element_type=jnp.float32) + jnp.dot(
-        weight_all[1], flat_real, preferred_element_type=jnp.float32
-    )
-    detected = (beam_real * beam_real + beam_imag * beam_imag) / inputs_all
-    channel_power = detected.reshape(-1, items, width)
-    return lax.all_to_all(channel_power, "stn", split_axis=0, concat_axis=2, tiled=True)
+    here = lax.axis_index("stn")
+    power = jnp.where(here % 2 == 1, power[:, :, ::-1], power)
+    power = jnp.where(here >= 16, power[::-1], power)
+    received = lax.all_to_all(power.reshape(32, 16, 128), "stn", 0, 0, tiled=True)
+    return received.transpose(1, 0, 2).reshape(16, 1, channels).astype(jnp.float32)
 
 
 def solution(mesh):

time: 153 us -> 143 us (0.935)
  starting transfers between devices: 8.71 us -> 49.8 us
  blocking collectives: 73.9 us -> 45.6 us
  between operations: 13.7 us -> 0.42 us
  local copies, waits for them, and re-layouts: 21.8 us -> 13 us
  matrix products: 14 us -> 17.2 us
  other arithmetic: 6.45 us -> 3.41 us
    all_to_all x3 -> x1, blocking collectives: 73.9 us -> 16.8 us  [on_device(): lax.all_to_all(power.reshape(32, 16, 128), 'stn', 0, 0, tiled=True)]
    all_gather x0 -> x1, blocking collectives: none -> 28.8 us  [on_device(): lax.all_gather(own, 'stn', axis=0, tiled=True, axis_index_groups=Z_GROUPS)]
    all_to_all x1 -> x2, starting transfers between devices: 8.67 us -> 29.5 us  [the longest x1 20.7 us: on_device(): lax.all_to_all(outgoing, BOTH, split_axis=0, concat_axis=0, tiled=True)]
    ppermute x0 -> x3, starting transfers between devices: none -> 20.3 us  [the longest x1 9.07 us: on_device(): other_core = lax.ppermute(gathered, 'stn', SWAP_CORE)]
    slice x4 -> x0, local copies, waits for them, and re-layouts: 5.8 us -> none  [the longest x1 5.55 us: on_device(): weight_all[1]]
    all_gather x1 -> x0, waiting for transfers between devices: 4.64 us -> none  [on_device(): weight_all = lax.all_gather(weight_low, 'stn', axis=1, tiled=True)]
    all_to_all x1 -> x2, waiting for transfers between devices: 7.69 us -> 12.3 us  [the longest x1 12.3 us: on_device(): lax.all_to_all(voltages, 'tm', split_axis=1, concat_axis=2, tiled=True)]
    all_to_all x4 -> x1, local copies, waits for them, and re-layouts: 3.91 us -> 0.29 us  [on_device(): lax.all_to_all(voltages, 'tm', split_axis=1, concat_axis=2, tiled=True)]
  transfers between devices with their start and end apart: 2 -> 5, of which waited for: 2 -> 2; matrix products, arithmetic and copies ran while one was open for 20% -> 3% of each run, Pallas kernels for 0% -> 0%
where the time goes in v1:
time: 143 us; the launch traced here: 142 us
  starting transfers between devices  49.8 us (35%)
  blocking collectives  45.6 us (32%)
  matrix products  17.2 us (12%)
  local copies, waits for them, and re-layouts  13 us (9%)
  waiting for transfers between devices  12.6 us (9%)
  other arithmetic  3.41 us (2%)
    all_gather x1, blocking collectives, on_device(): lax.all_gather(own, 'stn', axis=0, tiled=True, axis_index_groups=Z_GROUPS)  28.8 us
    all_to_all x1, starting transfers between devices, on_device(): lax.all_to_all(outgoing, BOTH, split_axis=0, concat_axis=0, tiled=True)  20.7 us
    all_to_all x1, blocking collectives, on_device(): lax.all_to_all(power.reshape(32, 16, 128), 'stn', 0, 0, tiled=True)  16.8 us
    all_to_all x1, waiting for transfers between devices, on_device(): lax.all_to_all(voltages, 'tm', split_axis=1, concat_axis=2, tiled=True)  12.3 us
    ppermute x1, starting transfers between devices, on_device(): other_core = lax.ppermute(gathered, 'stn', SWAP_CORE)  9.07 us
    all_to_all x1, starting transfers between devices, on_device(): lax.all_to_all(voltages, 'tm', split_axis=1, concat_axis=2, tiled=True)  8.8 us
    ppermute x1, starting transfers between devices, on_device(): other_both = lax.ppermute(other_xhi, 'stn', SWAP_CORE)  7.38 us
    ppermute x1, starting transfers between devices, on_device(): other_xhi = lax.ppermute(gathered, 'stn', SWAP_XHI)  3.86 us
  transfers between devices with their start and end apart: 5, of which 2 were waited for; matrix products, arithmetic and copies ran while one was open for 3% of the time, Pallas kernels for 0%

profile of v1, /device:TPU:1, one launch (start us, length us, event | category | flops | bytes accessed | tf_op | source)
XLA Modules:
  0.0 142.0 jit_solution(15188620609447460475)
XLA Ops:
  0.0 0.0 copy-start.5
  0.0 0.0 copy-start.3
  0.0 2.4 %copy.88 = bf16[2,32,4096]{2,0,1:T(2,128)(2,1)} copy(bf16[2,32,4096]{2,1,0:T(8,128)(2,1)} %param.5) | data formatting | bytes 1048576 | tf_op args[0]
  2.4 0.0 copy-start.2
  2.4 8.8 %all-to-all-start = ((bf16[2,32,4096]{2,0,1:T(2,128)(2,1)}), bf16[2,32,4096]{2,0,1:T(2,128)(2,1)S(1)}, u32[]{:S(2)}, u32[]{:S(2)}) async-start(bf16[2,32,4096]{2,0,1:T(2,128)(2,1)} %copy.88), calls=%async_computation | async-start | bytes 1048576 | tf_op jit(solution)/shard_map/all_to_all | solution.py:100
  11.2 0.1 fusion.56
  11.4 0.1 copy.94
  11.4 0.0 copy-done.5
  11.5 0.1 mul.421
  11.5 0.1 copy.87
  11.6 0.1 mul.423
  11.7 0.1 iota_add_fusion
  11.8 0.0 copy-done.3
  11.9 0.1 fusion.55
  12.0 0.1 copy.99
  12.1 0.0 copy-done.2
  12.1 0.1 fusion.107
  12.2 12.3 %all-to-all-done = bf16[2,32,4096]{2,0,1:T(2,128)(2,1)S(1)} async-done(((bf16[2,32,4096]{2,0,1:T(2,128)(2,1)}), bf16[2,32,4096]{2,0,1:T(2,128)(2,1)S(1)}, u32[]{:S(2)}, u32[]{:S(2)}) %all-to-all-start) | async-done | bytes 524320 | tf_op jit(solution)/shard_map/all_to_all | solution.py:100
  24.5 0.3 copy.148
  24.8 1.6 %multiply_add_fusion.1 = f32[2,2,16,4096]{3,2,1,0:T(8,128)S(1)} fusion(bf16[2,2,16,4096]{3,2,1,0:T(8,128)(2,1)S(1)} %bitcast.108, f32[4096]{0:T(1024)S(1)} %bitcast.126, f32[4096]{0:T(1024)S(1)} %bitcast.127, f32[4096]{0:T(1024)S(1)} %bitcast.117, f32[4096]{0:T(1024)S(1)} %bitcast.118, f32[4096]{0:T(1024)S(1)} %bitcast.119, f32[4096]{0:T(1024)S(1)} %bitcast.120, ...), kind=kLoop, calls=%fused_computation.29 | loop fusion | flops 9175040 | bytes 1769472 | tf_op jit(solution)/shard_map/add | solution.py:63
  26.4 0.1 fusion.106
  26.5 0.4 reshape_reshape_squeeze.7
  26.9 2.8 %fusion.49 = f32[32,64,64]{2,1,0:T(8,128)} fusion(f32[32,64,64]{2,1,0:T(8,128)S(1)} %reshape_reshape_squeeze.7), kind=kOutput, calls=%fused_computation.86 | convolution fusion | flops 100720640 | bytes 1048576 | tf_op jit(solution)/shard_map/pab,ak->pbk/dot_general | solution.py:40
  29.7 0.4 reshape_reshape_squeeze.6
  30.1 0.0 copy-start
  30.1 1.8 %fusion.51 = f32[32,64,64]{2,1,0:T(8,128)S(1)} fusion(f32[32,64,64]{2,1,0:T(8,128)S(1)} %reshape_reshape_squeeze.6), kind=kOutput, calls=%fused_computation.88 | convolution fusion | flops 100720640 | bytes 1048576 | tf_op jit(solution)/shard_map/pab,ak->pbk/dot_general | solution.py:37
  32.0 0.0 copy-done
  32.0 1.8 %convolution_subtract_fusion.1 = f32[32,64,64]{2,1,0:T(8,128)S(1)} fusion(f32[32,64,64]{2,1,0:T(8,128)S(1)} %copy-done, f32[32,64,64]{2,1,0:T(8,128)S(1)} %reshape_reshape_squeeze.6), kind=kOutput, calls=%fused_computation.20 | convolution fusion | flops 100851712 | bytes 1572864 | tf_op jit(solution)/shard_map/pab,ak->pbk/dot_general | solution.py:40
  33.8 1.8 %convolution_add_fusion.1 = f32[32,64,64]{2,1,0:T(8,128)S(1)} fusion(f32[32,64,64]{2,1,0:T(8,128)S(1)} %fusion.51, f32[32,64,64]{2,1,0:T(8,128)S(1)} %reshape_reshape_squeeze.7), kind=kOutput, calls=%fused_computation.21 | convolution fusion | flops 100851712 | bytes 1572864 | tf_op jit(solution)/shard_map/pab,ak->pbk/dot_general | solution.py:37
  35.6 1.2 fusion.20
  36.8 1.2 fusion.21
  38.0 2.2 %fusion.10 = bf16[32,64,64]{2,1,0:T(8,128)(2,1)} fusion(f32[64,32,64]{2,0,1:T(8,128)S(1)} %fusion.20, f32[32,64,64]{2,1,0:T(8,128)S(1)} %convolution_add_fusion.1, f32[32,64,64]{2,1,0:T(8,128)S(1)} %convolution_subtract_fusion.1, f32[64,64]{1,0:T(8,128)S(1)} %copy.99, f32[64,64]{1,0:T(8,128)S(1)} %copy.94), kind=kOutput, calls=%fused_computation.25 | convolution fusion | flops 101507072 | bytes 1867776 | tf_op jit(solution)/shard_map/pbk,bm->pmk/dot_general | solution.py:45
  40.2 3.1 %convert_element_type.190 = bf16[1,2,16,32,128]{4,0,3,2,1:T(2,128)(2,1)} reshape(bf16[32,64,64]{2,1,0:T(8,128)(2,1)} %fusion.10) | data formatting | bytes 524288 | tf_op jit(solution)/shard_map/convert_element_type | solution.py:69
  43.2 2.0 %fusion.9 = bf16[32,64,64]{2,1,0:T(8,128)(2,1)} fusion(f32[64,32,64]{2,0,1:T(8,128)S(1)} %fusion.21, f32[32,64,64]{2,1,0:T(8,128)S(1)} %convolution_subtract_fusion.1, f32[32,64,64]{2,1,0:T(8,128)S(1)} %convolution_add_fusion.1, f32[64,64]{1,0:T(8,128)S(1)} %copy.99, f32[64,64]{1,0:T(8,128)S(1)} %copy.94), kind=kOutput, calls=%fused_computation.24 | convolution fusion | flops 101507072 | bytes 1867776 | tf_op jit(solution)/shard_map/pbk,bm->pmk/dot_general | solution.py:48
  45.2 0.0 copy-start.1
  45.2 2.4 %convert_element_type.191 = bf16[1,2,16,32,128]{4,0,3,2,1:T(2,128)(2,1)S(1)} reshape(bf16[32,64,64]{2,1,0:T(8,128)(2,1)} %fusion.9) | data formatting | bytes 524288 | tf_op jit(solution)/shard_map/convert_element_type | solution.py:69
  47.7 0.0 copy-done.1
  47.7 1.2 maximum_bitcast_fusion
  48.9 0.3 reshape.380
  49.2 0.0 copy-start.4
  49.2 1.3 copy.102
  50.6 20.7 %all-to-all-start.1 = ((bf16[512,2,256]{2,1,0:T(2,128)(2,1)}), bf16[512,2,256]{2,1,0:T(2,128)(2,1)S(1)}, u32[]{:S(2)}, u32[]{:S(2)}) async-start(bf16[512,2,256]{2,1,0:T(2,128)(2,1)} %copy.102), calls=%async_computation.1 | async-start | bytes 1048576 | tf_op jit(solution)/shard_map/all_to_all | solution.py:111
  71.3 0.0 copy-done.4
  71.3 0.2 add.181
  71.5 0.1 broadcast_in_dim.2
  71.6 0.2 gt.17
  71.8 1.0 fusion.11
  72.8 28.8 %all_gather.3 = bf16[256,1024]{1,0:T(8,128)(2,1)S(1)} all-gather(bf16[32,1024]{1,0:T(8,128)(2,1)S(1)} %fusion.11), channel_id=1, replica_groups={{0,2,4,6,8,10,12,14},{1,3,5,7,9,11,13,15},{16,18,20,22,24,26,28,30},{17..., dimensions={0}, use_global_device_ids=true | all-gather | bytes 589824 | tf_op jit(solution)/shard_map/all_gather | solution.py:102
  101.6 3.9 %collective-permute-start.1 = (bf16[256,1024]{1,0:T(8,128)(2,1)S(1)}, bf16[256,1024]{1,0:T(8,128)(2,1)S(1)}, u32[]{:S(2)}, u32[]{:S(2)}) collective-permute-start(bf16[256,1024]{1,0:T(8,128)(2,1)S(1)} %all_gather.3), channel_id=1, source_target_pairs={{0,16},{1,17},{2,18},{3,19},{4,20},{5,21},{6,22},{7,23},{8,24},{9,... | collective-permute-start | bytes 1572872 | tf_op jit(solution)/shard_map/ppermute | solution.py:114
  105.5 9.1 %collective-permute-start = (bf16[256,1024]{1,0:T(8,128)(2,1)S(1)}, bf16[256,1024]{1,0:T(8,128)(2,1)S(1)}, u32[]{:S(2)}, u32[]{:S(2)}) collective-permute-start(bf16[256,1024]{1,0:T(8,128)(2,1)S(1)} %all_gather.3), channel_id=1, source_target_pairs={{0,1},{1,0},{2,3},{3,2},{4,5},{5,4},{6,7},{7,6},{8,9},{9,8},{10,11... | collective-permute-start | bytes 1572872 | tf_op jit(solution)/shard_map/ppermute | solution.py:113
  114.6 0.0 collective-permute-done.1
  114.6 7.4 %collective-permute-start.2 = (bf16[256,1024]{1,0:T(8,128)(2,1)S(1)}, bf16[256,1024]{1,0:T(8,128)(2,1)S(1)}, u32[]{:S(2)}, u32[]{:S(2)}) collective-permute-start(bf16[256,1024]{1,0:T(8,128)(2,1)S(1)} %collective-permute-done.1), channel_id=1, source_target_pairs={{0,1},{1,0},{2,3},{3,2},{4,5},{5,4},{6,7},{7,6},{8,9},{9,8},{10,11... | collective-permute-start | bytes 1572872 | tf_op jit(solution)/shard_map/ppermute | solution.py:115
  122.0 0.0 all-to-all-done.1
  122.0 0.2 reshape.381
  122.2 0.2 copy.103
  122.4 0.0 collective-permute-done
  122.4 0.3 fusion.18
  122.8 0.3 fusion.108
  123.2 0.3 collective-permute-done.2
  123.5 0.3 fusion.14
  123.8 0.3 fusion.16
  124.4 16.8 %all_to_all.25 = bf16[32,16,128]{2,1,0:T(8,128)(2,1)S(1)} all-to-all(bf16[32,16,128]{2,1,0:T(8,128)(2,1)S(1)} %bitcast.115), channel_id=1, replica_groups=mesh['tm'=16,'stn'=32] {'stn'}, dimensions={0} | all-to-all | bytes 262144 | tf_op jit(solution)/shard_map/all_to_all | solution.py:125
  141.2 0.8 copy.118
  (13 shorter events, 0.2 us)
Async XLA Ops:
  0.0 11.4 %copy-start.5 = (s32[512]{0:T(512)S(1)}, s32[512]{0:T(512)}, u32[]{:S(2)}) copy-start(s32[512]{0:T(512)} %param.8) | copy-start | bytes 6148
  0.0 11.8 %copy-start.3 = (s32[2,16,1024]{2,1,0:T(8,128)S(1)}, s32[2,16,1024]{2,1,0:T(8,128)}, u32[]{:S(2)}) copy-start(s32[2,16,1024]{2,1,0:T(8,128)} %param.7) | copy-start | bytes 393220
  2.4 9.7 %copy-start.2 = (f32[12,4096]{1,0:T(8,128)S(1)}, f32[12,4096]{1,0:T(8,128)}, u32[]{:S(2)}) copy-start(f32[12,4096]{1,0:T(8,128)} %param.6) | copy-start | bytes 589828
  2.4 22.1 %all-to-all-start = ((bf16[2,32,4096]{2,0,1:T(2,128)(2,1)}), bf16[2,32,4096]{2,0,1:T(2,128)(2,1)S(1)}, u32[]{:S(2)}, u32[]{:S(2)}) async-start(bf16[2,32,4096]{2,0,1:T(2,128)(2,1)} %copy.88), calls=%async_computation | async-start | bytes 1048576 | tf_op jit(solution)/shard_map/all_to_all | solution.py:100
  30.1 1.8 %copy-start = (f32[32,64,64]{2,1,0:T(8,128)S(1)}, f32[32,64,64]{2,1,0:T(8,128)}, u32[]{:S(2)}) copy-start(f32[32,64,64]{2,1,0:T(8,128)} %fusion.49) | copy-start | bytes 1572868
  45.2 2.4 %copy-start.1 = (bf16[1,2,16,32,128]{4,0,3,2,1:T(2,128)(2,1)S(1)}, bf16[1,2,16,32,128]{4,0,3,2,1:T(2,128)(2,1)}, u32[]{:S(2)}) copy-start(bf16[1,2,16,32,128]{4,0,3,2,1:T(2,128)(2,1)} %convert_element_type.190) | copy-start | bytes 786436
  49.2 22.1 %copy-start.4 = (s32[512]{0:T(512)S(1)}, s32[512]{0:T(512)}, u32[]{:S(2)}) copy-start(s32[512]{0:T(512)} %param.9) | copy-start | bytes 6148
  50.6 71.4 %all-to-all-start.1 = ((bf16[512,2,256]{2,1,0:T(2,128)(2,1)}), bf16[512,2,256]{2,1,0:T(2,128)(2,1)S(1)}, u32[]{:S(2)}, u32[]{:S(2)}) async-start(bf16[512,2,256]{2,1,0:T(2,128)(2,1)} %copy.102), calls=%async_computation.1 | async-start | bytes 1048576 | tf_op jit(solution)/shard_map/all_to_all | solution.py:111
  101.6 13.0 %collective-permute-start.1 = (bf16[256,1024]{1,0:T(8,128)(2,1)S(1)}, bf16[256,1024]{1,0:T(8,128)(2,1)S(1)}, u32[]{:S(2)}, u32[]{:S(2)}) collective-permute-start(bf16[256,1024]{1,0:T(8,128)(2,1)S(1)} %all_gather.3), channel_id=1, source_target_pairs={{0,16},{1,17},{2,18},{3,19},{4,20},{5,21},{6,22},{7,23},{8,24},{9,... | collective-permute-start | bytes 1572872 | tf_op jit(solution)/shard_map/ppermute | solution.py:114
  105.5 16.9 %collective-permute-start = (bf16[256,1024]{1,0:T(8,128)(2,1)S(1)}, bf16[256,1024]{1,0:T(8,128)(2,1)S(1)}, u32[]{:S(2)}, u32[]{:S(2)}) collective-permute-start(bf16[256,1024]{1,0:T(8,128)(2,1)S(1)} %all_gather.3), channel_id=1, source_target_pairs={{0,1},{1,0},{2,3},{3,2},{4,5},{5,4},{6,7},{7,6},{8,9},{9,8},{10,11... | collective-permute-start | bytes 1572872 | tf_op jit(solution)/shard_map/ppermute | solution.py:113
  114.6 8.9 %collective-permute-start.2 = (bf16[256,1024]{1,0:T(8,128)(2,1)S(1)}, bf16[256,1024]{1,0:T(8,128)(2,1)S(1)}, u32[]{:S(2)}, u32[]{:S(2)}) collective-permute-start(bf16[256,1024]{1,0:T(8,128)(2,1)S(1)} %collective-permute-done.1), channel_id=1, source_target_pairs={{0,1},{1,0},{2,3},{3,2},{4,5},{5,4},{6,7},{7,6},{8,9},{9,8},{10,11... | collective-permute-start | bytes 1572872 | tf_op jit(solution)/shard_map/ppermute | solution.py:115

commit v2 on v1

v2 whole, which is shorter than its diff:
```python
import math

import jax
import jax.numpy as jnp
import numpy as np
from jax import lax
from jax.experimental import pallas as pl
from jax.experimental.pallas import tpu as pltpu
from jax.sharding import PartitionSpec as P

BOTH = ("tm", "stn")
LANES = 128
FRAMES = 16
OUTER = 32
TAPS = 12


def stn_index(xhi, z, core):
    return xhi * 16 + z * 2 + core


QUADS = [
    [stn_index(xhi, 4 * half + z, core) for z in range(4)]
    for xhi in range(2)
    for half in range(2)
    for core in range(2)
]
SWAP_XHI = [(i, i ^ 16) for i in range(32)]
SWAP_HALF = [(i, i ^ 8) for i in range(32)]
SWAP_CORE = [(i, i ^ 1) for i in range(32)]


def dft_tables(channels):
    b = np.arange(LANES, dtype=np.float64)
    k1 = np.arange(OUTER, dtype=np.float64)
    turn = 2.0 * np.pi * k1[:, None] * b[None, :] / channels
    twiddle = np.stack([np.cos(turn), np.sin(turn)]).astype(np.float32)
    inner = 2.0 * np.pi * ((b[:, None] * b[None, :]) % LANES) / LANES
    scale = 1.0 / math.sqrt(channels)
    table = (np.concatenate([np.cos(inner), np.sin(inner)]) * scale).astype(np.float32)
    return twiddle, table


def times(value, angle):
    real, imag = value
    cosine, sine = math.cos(angle), math.sin(angle)
    if abs(sine) < 1e-12:
        return (real, imag) if cosine > 0 else (-real, -imag)
    if abs(cosine) < 1e-12:
        return (imag, -real) if sine > 0 else (-imag, real)
    if abs(abs(cosine) - abs(sine)) < 1e-12:
        sign_c = 1.0 if cosine > 0 else -1.0
        sign_s = 1.0 if sine > 0 else -1.0
        root = abs(cosine)
        return (real * sign_c + imag * sign_s) * root, (imag * sign_c - real * sign_s) * root
    return real * cosine + imag * sine, imag * cosine - real * sine


def plus(first, second):
    return first[0] + second[0], first[1] + second[1]


def minus(first, second):
    return first[0] - second[0], first[1] - second[1]


def dft_small(values):
    size = len(values)
    if size == 1:
        return values
    half = size // 2
    even = dft_small([plus(values[j], values[j + half]) for j in range(half)])
    odd = dft_small(
        [times(minus(values[j], values[j + half]), 2.0 * math.pi * j / size) for j in range(half)]
    )
    out = []
    for j in range(half):
        out += [even[j], odd[j]]
    return out


def spectra_kernel(
    frames_ref, taps_ref, twiddle_ref, high_ref, low_ref, gate_ref, out_ref,
    padded, filtered, first_half, second_half,
):
    del gate_ref
    blank = jnp.zeros((FRAMES, LANES), jnp.float32)

    def fir(a, carry):
        lane = pl.ds(pl.multiple_of(a * LANES, LANES), LANES)
        for part in range(2):
            for i in range(2):
                row = 2 * part + i
                padded[row, a, pl.ds(0, FRAMES), :] = blank
                padded[row, a, pl.ds(FRAMES, FRAMES), :] = frames_ref[part, i, :, lane].astype(
                    jnp.float32
                )
        totals = [blank] * 4
        for t in range(TAPS):
            tap = taps_ref[t, pl.ds(a, 1), :]
            for row in range(4):
                window = padded[row, a, pl.ds(FRAMES - TAPS + 1 + t, FRAMES), :]
                totals[row] = totals[row] + window * tap
        for part in range(2):
            for i in range(2):
                filtered[part, a, pl.ds(FRAMES * i, FRAMES), :] = totals[2 * part + i]
        return carry

    lax.fori_loop(0, OUTER, fir, 0)

    def load(a, i):
        rows = pl.ds(FRAMES * i, FRAMES)
        return filtered[0, a, rows, :], filtered[1, a, rows, :]

    for i in range(2):
        rows = pl.ds(FRAMES * i, FRAMES)
        for a0 in range(8):
            spread = dft_small([load(8 * a1 + a0, i) for a1 in range(4)])
            for j in range(4):
                real, imag = times(spread[j], 2.0 * math.pi * a0 * j / OUTER)
                filtered[0, 8 * j + a0, rows, :] = real
                filtered[1, 8 * j + a0, rows, :] = imag
    for i in range(2):
        for j in range(4):
            spread = dft_small([load(8 * j + a0, i) for a0 in range(8)])
            for m in range(8):
                k1 = j + 4 * m
                cosine = twiddle_ref[0, pl.ds(k1, 1), :]
                sine = twiddle_ref[1, pl.ds(k1, 1), :]
                real, imag = spread[m]
                turned_real = real * cosine + imag * sine
                turned_imag = imag * cosine - real * sine
                upper = pl.ds(4 * k1 + i, FRAMES, stride=4 * OUTER)
                lower = pl.ds(4 * k1 + 2 + i, FRAMES, stride=4 * OUTER)
                first_half[upper, :] = turned_real
                second_half[upper, :] = turned_imag
                first_half[lower, :] = turned_imag
                second_half[lower, :] = -turned_real

    block = 256

    def product(step, carry):
        rows = pl.ds(pl.multiple_of(step * block, block), block)
        left = jnp.concatenate([first_half[rows, :], second_half[rows, :]], axis=1)
        left_high = left.astype(jnp.bfloat16)
        left_low = (left - left_high.astype(jnp.float32)).astype(jnp.bfloat16)
        right_high = high_ref[...]
        total = jnp.dot(left_high, right_high, preferred_element_type=jnp.float32)
        total += jnp.dot(left_low, right_high, preferred_element_type=jnp.float32)
        total += jnp.dot(left_high, low_ref[...], preferred_element_type=jnp.float32)
        out_ref[rows, :] = total.astype(jnp.bfloat16)
        return carry

    lax.fori_loop(0, 4 * OUTER * FRAMES // block, product, 0)


def spectra_of(frames, filter_taps, gate):
    channels = frames.shape[3]
    twiddle, table = dft_tables(channels)
    high = table.astype(jnp.bfloat16)
    low = (table - high.astype(np.float32)).astype(jnp.bfloat16)
    rows = 4 * OUTER * FRAMES
    return pl.pallas_call(
        spectra_kernel,
        out_shape=jax.ShapeDtypeStruct((rows, LANES), jnp.bfloat16),
        in_specs=[pl.BlockSpec(memory_space=pltpu.VMEM)] * 5 + [pl.BlockSpec(memory_space=pl.ANY)],
        out_specs=pl.BlockSpec(memory_space=pltpu.VMEM),
        scratch_shapes=[
            pltpu.VMEM((4, OUTER, 2 * FRAMES, LANES), jnp.float32),
            pltpu.VMEM((2, OUTER, 2 * FRAMES, LANES), jnp.float32),
            pltpu.VMEM((rows, LANES), jnp.float32),
            pltpu.VMEM((rows, LANES), jnp.float32),
        ],
        compiler_params=pltpu.CompilerParams(vmem_limit_bytes=24 * 1024 * 1024),
        cost_estimate=pl.CostEstimate(
            flops=6 * rows * 256 * LANES, bytes_accessed=4 * 1024 * 1024, transcendentals=0
        ),
        name="spectra",
    )(
        frames,
        filter_taps.reshape(TAPS, OUTER, LANES),
        jnp.asarray(twiddle),
        jnp.asarray(high),
        jnp.asarray(low),
        gate,
    )


def local_weights(beam_weights, station_map, station_flags):
    beams = beam_weights.shape[1]
    inputs = beam_weights.shape[2]
    order = station_map.reshape(32, 16).T.reshape(-1)
    target = (2 * order[:, None] + jnp.arange(2, dtype=jnp.int32)[None, :]).reshape(-1)
    keep = jnp.repeat(station_flags, 2)
    rows = jnp.arange(inputs, dtype=jnp.int32)
    select = ((rows[:, None] == target[None, :]) & (keep[:, None] > 0)).astype(jnp.bfloat16)
    weight_low = (beam_weights.astype(jnp.float32) * (1.0 / 32768.0)).astype(jnp.bfloat16)
    return jnp.dot(
        weight_low.reshape(2 * beams, inputs), select, preferred_element_type=jnp.float32
    ).astype(jnp.bfloat16)


def block_power(weights, spectra, inputs_all):
    product = jnp.dot(weights, spectra, preferred_element_type=jnp.float32)
    product = product.reshape(8, 2, 16, 2, LANES)
    beam_real = product[:, 0, :, 0] - product[:, 1, :, 1]
    beam_imag = product[:, 0, :, 1] + product[:, 1, :, 0]
    return ((beam_real * beam_real + beam_imag * beam_imag) / inputs_all).astype(jnp.bfloat16)


def channel_order(received):
    by_beam = received.transpose(1, 0, 2)
    lanes = np.arange(LANES)
    keep = (lanes[:, None] // OUTER == lanes[None, :] % 4).astype(np.float32)
    pick = (np.arange(OUTER)[:, None] == lanes[None, :] // 4).astype(np.float32)
    spread = jnp.tile(by_beam, (1, 4, 1)) * jnp.asarray(keep, jnp.bfloat16)[None]
    return jnp.einsum(
        "jk,bqk->bjq", jnp.asarray(pick, jnp.bfloat16), spread, preferred_element_type=jnp.float32
    )


def on_device(voltages, filter_taps, beam_weights, station_map, station_flags):
    channels = filter_taps.shape[1]
    inputs_all = beam_weights.shape[2]
    here = lax.axis_index("stn")
    retiled = lax.all_to_all(voltages, "tm", split_axis=1, concat_axis=2, tiled=True)
    own = local_weights(beam_weights, station_map, station_flags)
    far = lax.ppermute(own, "stn", SWAP_HALF)
    upper = (here // 8) % 2 == 1
    both = jnp.concatenate([jnp.where(upper, far, own), jnp.where(upper, own, far)], axis=0)
    gathered = lax.all_gather(both, "stn", axis=0, tiled=True, axis_index_groups=QUADS)
    frames = retiled.reshape(2, 2, FRAMES, channels)
    outgoing = spectra_of(frames, filter_taps, gathered[:16, :LANES]).reshape(512, 4, LANES)
    turned = lax.all_to_all(outgoing, BOTH, split_axis=0, concat_axis=0, tiled=True)
    turned = turned.reshape(512, 2, 2, LANES).transpose(0, 2, 1, 3).reshape(inputs_all, 2 * LANES)
    other_core = lax.ppermute(gathered, "stn", SWAP_CORE)
    other_xhi = lax.ppermute(gathered, "stn", SWAP_XHI)
    other_both = lax.ppermute(other_xhi, "stn", SWAP_CORE)
    power = jnp.stack(
        [
            block_power(weights, turned, inputs_all)
            for weights in (gathered, other_core, other_xhi, other_both)
        ]
    ).reshape(2, 2, 4, 2, 16, LANES)
    power = power.transpose(0, 3, 2, 1, 4, 5)
    power = jnp.where(here % 2 == 1, power[:, :, :, ::-1], power)
    power = jnp.where(here >= 16, power[::-1], power)
    received = lax.all_to_all(power.reshape(32, 16, LANES), "stn", 0, 0, tiled=True)
    return channel_order(received).reshape(16, 1, channels)


def solution(mesh):
    placed = (P(None, "stn", "tm"), P(), P(None, "stn", None), P(), P())
    return jax.shard_map(
        on_device, mesh=mesh, in_specs=placed, out_specs=P("stn", "tm", None), check_vma=False
    )
```

time: 143 us -> 114 us (0.80)
  blocking collectives: 45.6 us -> 30.4 us
  matrix products: 17.2 us -> 3.37 us
  local copies, waits for them, and re-layouts: 13 us -> 5.7 us
  Pallas kernels: 0 us -> 6.24 us
  waiting for transfers between devices: 12.6 us -> 15.8 us
  other arithmetic: 3.41 us -> 0.4 us
  starting transfers between devices: 49.8 us -> 51.3 us
    all_gather x1, blocking collectives: 28.8 us -> 14.8 us  [on_device(): lax.all_gather(both, 'stn', axis=0, tiled=True, axis_index_groups=QUADS)]
    all_to_all x1, waiting for transfers between devices: 0.01 us -> 14 us  [on_device(): lax.all_to_all(outgoing, BOTH, split_axis=0, concat_axis=0, tiled=True)]
    dot_general x8 -> x1, matrix products: 14.8 us -> 0.98 us  [channel_order(): jnp.einsum('jk,bqk->bjq', jnp.asarray(pick, jnp.bfloat16), spread, prefer...]
    all_to_all x1, waiting for transfers between devices: 12.3 us -> 0.01 us  [on_device(): lax.all_to_all(voltages, 'tm', split_axis=1, concat_axis=2, tiled=True)]
    ppermute x0 -> x1, starting transfers between devices: none -> 10.6 us  [on_device(): far = lax.ppermute(own, 'stn', SWAP_HALF)]
    ppermute x1, starting transfers between devices: 9.07 us -> 1.92 us  [on_device(): other_core = lax.ppermute(gathered, 'stn', SWAP_CORE)]
    convert_element_type x3 -> x0, local copies, waits for them, and re-layouts: 6.28 us -> none  [the longest x1 3.07 us: filter_spectra(): chan_real.astype(jnp.bfloat16)]
    pallas_call x0 -> x1, Pallas kernels: none -> 6.24 us  [spectra_of(): pl.pallas_call(spectra_kernel, out_shape=jax.ShapeDtypeStruct((rows, LANE...]
  transfers between devices with their start and end apart: 5 -> 6, of which waited for: 2 -> 2; matrix products, arithmetic and copies ran while one was open for 3% -> 3% of each run, Pallas kernels for 0% -> 5%
where the time goes in v2:
time: 114 us
  starting transfers between devices  51.3 us (45%)
  blocking collectives  30.4 us (27%)
  waiting for transfers between devices  15.8 us (14%)
  Pallas kernels  6.24 us (5%)
  local copies, waits for them, and re-layouts  5.7 us (5%)
  matrix products  3.37 us (3%)
    all_to_all x1, starting transfers between devices, on_device(): lax.all_to_all(outgoing, BOTH, split_axis=0, concat_axis=0, tiled=True)  19.4 us
    all_to_all x1, blocking collectives, on_device(): lax.all_to_all(power.reshape(32, 16, LANES), 'stn', 0, 0, tiled=True)  15.6 us
    all_gather x1, blocking collectives, on_device(): lax.all_gather(both, 'stn', axis=0, tiled=True, axis_index_groups=QUADS)  14.8 us
    all_to_all x1, waiting for transfers between devices, on_device(): lax.all_to_all(outgoing, BOTH, split_axis=0, concat_axis=0, tiled=True)  14 us
    ppermute x1, starting transfers between devices, on_device(): far = lax.ppermute(own, 'stn', SWAP_HALF)  10.6 us
    all_to_all x1, starting transfers between devices, on_device(): lax.all_to_all(voltages, 'tm', split_axis=1, concat_axis=2, tiled=True)  8.8 us
    pallas_call x1, Pallas kernels, spectra_of(): pl.pallas_call(spectra_kernel, out_shape=jax.ShapeDtypeStruct((rows, LANE...  6.24 us
    ppermute x1, starting transfers between devices, on_device(): other_both = lax.ppermute(other_xhi, 'stn', SWAP_CORE)  6.21 us
  transfers between devices with their start and end apart: 6, of which 2 were waited for; matrix products, arithmetic and copies ran while one was open for 3% of the time, Pallas kernels for 5%

profile of v2, /device:TPU:1, one launch (start us, length us, event | category | flops | bytes accessed | tf_op | source)
XLA Modules:
  0.0 113.6 jit_solution(3140891932558701682)
XLA Ops:
  0.0 2.4 %copy.69 = bf16[2,32,4096]{2,0,1:T(2,128)(2,1)} copy(bf16[2,32,4096]{2,1,0:T(8,128)(2,1)} %param.10) | data formatting | bytes 1048576 | tf_op args[0]
  2.4 0.0 copy-start.8
  2.4 8.8 %all-to-all-start = ((bf16[2,32,4096]{2,0,1:T(2,128)(2,1)}), bf16[2,32,4096]{2,0,1:T(2,128)(2,1)S(1)}, u32[]{:S(2)}, u32[]{:S(2)}) async-start(bf16[2,32,4096]{2,0,1:T(2,128)(2,1)} %copy.69), calls=%async_computation | async-start | bytes 1048576 | tf_op jit(solution)/shard_map/all_to_all | solution.py:226
  11.2 0.0 copy-done.8
  11.2 0.0 copy-start.7
  11.2 0.0 copy-start.4
  11.2 0.1 mul.126
  11.3 0.1 copy.68
  11.4 0.1 mul.128
  11.5 0.1 iota_add_fusion
  11.6 0.2 add.121
  11.8 0.1 copy-done.7
  11.9 0.1 broadcast_in_dim.2
  12.0 0.2 gt.17
  12.2 0.0 copy-done.4
  12.3 0.0 copy-start.3
  12.3 1.0 fusion.5
  13.3 10.6 %collective-permute-start = (bf16[32,1024]{1,0:T(8,128)(2,1)S(1)}, bf16[32,1024]{1,0:T(8,128)(2,1)S(1)}, u32[]{:S(2)}, u32[]{:S(2)}) collective-permute-start(bf16[32,1024]{1,0:T(8,128)(2,1)S(1)} %fusion.5), channel_id=1, source_target_pairs={{0,8},{1,9},{2,10},{3,11},{4,12},{5,13},{6,14},{7,15},{8,0},{9,1},... | collective-permute-start | bytes 196616 | tf_op jit(solution)/shard_map/ppermute | solution.py:228
  24.0 0.0 copy-done.3
  24.0 0.1 copy.99
  24.1 1.8 %collective-permute-done = bf16[32,1024]{1,0:T(8,128)(2,1)S(1)} collective-permute-done((bf16[32,1024]{1,0:T(8,128)(2,1)S(1)}, bf16[32,1024]{1,0:T(8,128)(2,1)S(1)}, u32[]{:S(2)}, u32[]{:S(2)}) %collective-permute-start) | collective-permute-done | bytes 65568 | tf_op jit(solution)/shard_map/ppermute | solution.py:228
  25.9 14.8 %all_gather.3 = bf16[256,1024]{1,0:T(8,128)(2,1)S(1)} all-gather(bf16[64,1024]{1,0:T(8,128)(2,1)S(1)} %pad_maximum_fusion), channel_id=1, replica_groups={{0,2,4,6},{1,3,5,7},{8,10,12,14},{9,11,13,15},{16,18,20,22},{17,19,21,2..., dimensions={0}, use_global_device_ids=true | all-gather | bytes 655360 | tf_op jit(solution)/shard_map/all_gather | solution.py:231
  40.7 4.3 %collective-permute-start.2 = (bf16[256,1024]{1,0:T(8,128)(2,1)S(1)}, bf16[256,1024]{1,0:T(8,128)(2,1)S(1)}, u32[]{:S(2)}, u32[]{:S(2)}) collective-permute-start(bf16[256,1024]{1,0:T(8,128)(2,1)S(1)} %all_gather.3), channel_id=1, source_target_pairs={{0,16},{1,17},{2,18},{3,19},{4,20},{5,21},{6,22},{7,23},{8,24},{9,... | collective-permute-start | bytes 1572872 | tf_op jit(solution)/shard_map/ppermute | solution.py:237
  45.0 0.0 all-to-all-done
  45.1 0.0 copy-start
  45.1 0.0 copy-start.1
  45.1 0.0 copy-start.2
  45.1 0.3 copy.111
  45.4 0.5 copy-done
  45.9 0.0 copy-done.1
  45.9 0.0 copy-done.2
  45.9 6.2 %spectra.1 = bf16[2048,128]{1,0:T(8,128)(2,1)} custom-call(bf16[2,2,16,4096]{3,2,1,0:T(8,128)(2,1)S(1)} %bitcast.74, f32[12,32,128]{2,1,0:T(8,128)S(1)} %slice.85.taps_ref, f32[2,32,128]{2,1,0:T(8,128)S(1)} %copy-done.2, bf16[256,128]{1,0:T(8,128)(2,1)S(1)} %copy-done, bf16[256,128]{1,0:T(8,128)(2,1)S(1)} %copy-done.1, bf16[16,128]{1,0:T(8,128)(2,1)S(1)} %slice.68.gate_ref), custom_call_target="tpu_custom_call" | custom-call | flops 402653184 | bytes 4194304 | tf_op jit(solution)/shard_map/spectra/pallas_call | solution.py:163
  52.2 19.4 %all-to-all-start.1 = ((bf16[512,4,128]{2,1,0:T(4,128)(2,1)}), bf16[512,4,128]{2,1,0:T(4,128)(2,1)S(1)}, u32[]{:S(2)}, u32[]{:S(2)}) async-start(bf16[512,4,128]{2,1,0:T(4,128)(2,1)} %bitcast.7), calls=%async_computation.1 | async-start | bytes 1048576 | tf_op jit(solution)/shard_map/all_to_all | solution.py:234
  71.6 0.0 collective-permute-done.2
  71.6 6.2 %collective-permute-start.3 = (bf16[256,1024]{1,0:T(8,128)(2,1)S(1)}, bf16[256,1024]{1,0:T(8,128)(2,1)S(1)}, u32[]{:S(2)}, u32[]{:S(2)}) collective-permute-start(bf16[256,1024]{1,0:T(8,128)(2,1)S(1)} %collective-permute-done.2), channel_id=1, source_target_pairs={{0,1},{1,0},{2,3},{3,2},{4,5},{5,4},{6,7},{7,6},{8,9},{9,8},{10,11... | collective-permute-start | bytes 1572872 | tf_op jit(solution)/shard_map/ppermute | solution.py:238
  77.8 1.9 %collective-permute-start.1 = (bf16[256,1024]{1,0:T(8,128)(2,1)S(1)}, bf16[256,1024]{1,0:T(8,128)(2,1)S(1)}, u32[]{:S(2)}, u32[]{:S(2)}) collective-permute-start(bf16[256,1024]{1,0:T(8,128)(2,1)S(1)} %all_gather.3), channel_id=1, source_target_pairs={{0,1},{1,0},{2,3},{3,2},{4,5},{5,4},{6,7},{7,6},{8,9},{9,8},{10,11... | collective-permute-start | bytes 1572872 | tf_op jit(solution)/shard_map/ppermute | solution.py:236
  79.8 14.0 %all-to-all-done.1 = bf16[512,4,128]{2,1,0:T(4,128)(2,1)S(1)} async-done(((bf16[512,4,128]{2,1,0:T(4,128)(2,1)}), bf16[512,4,128]{2,1,0:T(4,128)(2,1)S(1)}, u32[]{:S(2)}, u32[]{:S(2)}) %all-to-all-start.1) | async-done | bytes 524320 | tf_op jit(solution)/shard_map/all_to_all | solution.py:234
  93.7 0.1 copy.71
  93.8 0.5 copy.72
  94.3 0.1 copy.110
  94.4 0.2 copy.73
  94.7 0.0 collective-permute-done.3
  94.7 0.3 fusion.8
  95.0 0.0 collective-permute-done.1
  95.0 0.3 fusion.12
  95.4 0.3 fusion.10
  95.7 0.3 fusion.38
  96.2 0.0 copy-start.5
  96.3 15.6 %all_to_all.25 = bf16[32,16,128]{2,1,0:T(8,128)(2,1)S(1)} all-to-all(bf16[32,16,128]{2,1,0:T(8,128)(2,1)S(1)} %bitcast.90), channel_id=1, replica_groups=mesh['tm'=16,'stn'=32] {'stn'}, dimensions={0} | all-to-all | bytes 262144 | tf_op jit(solution)/shard_map/all_to_all | solution.py:248
  111.9 0.0 copy-start.6
  112.0 0.0 copy-done.5
  112.0 0.6 copy-done.6
  112.6 1.0 fusion.39
  (16 shorter events, 0.3 us)
Async XLA Ops:
  2.4 8.8 %copy-start.8 = (s32[512]{0:T(512)S(1)}, s32[512]{0:T(512)}, u32[]{:S(2)}) copy-start(s32[512]{0:T(512)} %param.13) | copy-start | bytes 6148
  2.4 42.7 %all-to-all-start = ((bf16[2,32,4096]{2,0,1:T(2,128)(2,1)}), bf16[2,32,4096]{2,0,1:T(2,128)(2,1)S(1)}, u32[]{:S(2)}, u32[]{:S(2)}) async-start(bf16[2,32,4096]{2,0,1:T(2,128)(2,1)} %copy.69), calls=%async_computation | async-start | bytes 1048576 | tf_op jit(solution)/shard_map/all_to_all | solution.py:226
  11.2 0.7 copy-start.7
  11.2 1.0 copy-start.4
  12.3 11.7 %copy-start.3 = (f32[12,4096]{1,0:T(8,128)S(1)}, f32[12,4096]{1,0:T(8,128)}, u32[]{:S(2)}) copy-start(f32[12,4096]{1,0:T(8,128)} %param.11) | copy-start | bytes 589828
  13.3 12.6 %collective-permute-start = (bf16[32,1024]{1,0:T(8,128)(2,1)S(1)}, bf16[32,1024]{1,0:T(8,128)(2,1)S(1)}, u32[]{:S(2)}, u32[]{:S(2)}) collective-permute-start(bf16[32,1024]{1,0:T(8,128)(2,1)S(1)} %fusion.5), channel_id=1, source_target_pairs={{0,8},{1,9},{2,10},{3,11},{4,12},{5,13},{6,14},{7,15},{8,0},{9,1},... | collective-permute-start | bytes 196616 | tf_op jit(solution)/shard_map/ppermute | solution.py:228
  40.7 30.9 %collective-permute-start.2 = (bf16[256,1024]{1,0:T(8,128)(2,1)S(1)}, bf16[256,1024]{1,0:T(8,128)(2,1)S(1)}, u32[]{:S(2)}, u32[]{:S(2)}) collective-permute-start(bf16[256,1024]{1,0:T(8,128)(2,1)S(1)} %all_gather.3), channel_id=1, source_target_pairs={{0,16},{1,17},{2,18},{3,19},{4,20},{5,21},{6,22},{7,23},{8,24},{9,... | collective-permute-start | bytes 1572872 | tf_op jit(solution)/shard_map/ppermute | solution.py:237
  45.1 0.8 copy-start
  45.1 0.9 copy-start.1
  45.1 0.9 copy-start.2
  52.2 41.6 %all-to-all-start.1 = ((bf16[512,4,128]{2,1,0:T(4,128)(2,1)}), bf16[512,4,128]{2,1,0:T(4,128)(2,1)S(1)}, u32[]{:S(2)}, u32[]{:S(2)}) async-start(bf16[512,4,128]{2,1,0:T(4,128)(2,1)} %bitcast.7), calls=%async_computation.1 | async-start | bytes 1048576 | tf_op jit(solution)/shard_map/all_to_all | solution.py:234
  71.6 23.1 %collective-permute-start.3 = (bf16[256,1024]{1,0:T(8,128)(2,1)S(1)}, bf16[256,1024]{1,0:T(8,128)(2,1)S(1)}, u32[]{:S(2)}, u32[]{:S(2)}) collective-permute-start(bf16[256,1024]{1,0:T(8,128)(2,1)S(1)} %collective-permute-done.2), channel_id=1, source_target_pairs={{0,1},{1,0},{2,3},{3,2},{4,5},{5,4},{6,7},{7,6},{8,9},{9,8},{10,11... | collective-permute-start | bytes 1572872 | tf_op jit(solution)/shard_map/ppermute | solution.py:238
  77.8 17.2 %collective-permute-start.1 = (bf16[256,1024]{1,0:T(8,128)(2,1)S(1)}, bf16[256,1024]{1,0:T(8,128)(2,1)S(1)}, u32[]{:S(2)}, u32[]{:S(2)}) collective-permute-start(bf16[256,1024]{1,0:T(8,128)(2,1)S(1)} %all_gather.3), channel_id=1, source_target_pairs={{0,1},{1,0},{2,3},{3,2},{4,5},{5,4},{6,7},{7,6},{8,9},{9,8},{10,11... | collective-permute-start | bytes 1572872 | tf_op jit(solution)/shard_map/ppermute | solution.py:236
  96.2 15.7 %copy-start.5 = (bf16[128,128]{1,0:T(8,128)(2,1)S(1)}, bf16[128,128]{1,0:T(8,128)(2,1)}, u32[]{:S(2)}) copy-start(bf16[128,128]{1,0:T(8,128)(2,1)} %constant.61.clone) | copy-start | bytes 98308
  111.9 0.7 copy-start.6
